TPU v7x, 128 devices: a whole 4x4x4 slice. The times are simulated.
128 devices in a mesh: dp: 8 (over z_hi, y), tensor: 16 (over z_lo, x, core).
Axes of the slice: x: 4, y: 4, z: 4 (z_hi: 2, z_lo: 2; z = z_hi * 2 + z_lo), core: 2. Of those that a mesh axis runs over, the one named last changes fastest.
Arguments:
- normed_input: bfloat16 [8192, 8192], P('dp', 'tensor'), may hold values from -6 to 6
- positions: int32 [8192], P('dp'), may hold values from 0 to 8191
- fixed_weight_matrix: bfloat16 [8192, 10240], P('dp', 'tensor'), may hold values from -0.09375 to 0.09375
- adapter_down_map: bfloat16 [8192, 16], P('tensor'), may hold values from -0.0625 to 0.0625
- adapter_up_map: bfloat16 [16, 10240], P(None, 'tensor'), may hold values from -0.0625 to 0.0625
- output_gradient: bfloat16 [8192, 10240], P('dp', 'tensor'), may hold values from -6 to 6
Outputs:
- grad_x: bfloat16 [8192, 8192], P('dp', 'tensor')
- grad_a: float32 [8192, 16], P('tensor')
- grad_b: float32 [16, 10240], P(None, 'tensor')
All inputs are finite; a program needn't handle non-finite values.
Results may differ from a plain program's by a relative error of at most 0.0048.
Values may be sent and summed in bfloat16 or wider, within the bound.
No kernel may reach another device: no remote copies, remote signals or barrier semaphores. Data moves between devices by JAX's collectives and lax.ppermute only.
A program may use at most 256 MiB of HBM per device.

v0:
```python
import math
import jax
import jax.numpy as jnp
from jax import lax
from jax.sharding import PartitionSpec as P

MODEL_WIDTH = 8192
KV = 1024
HEAD = 128


def copy_for_each(value, axis):
    peers = lax.axis_size(axis)
    return lax.all_to_all(
        jnp.broadcast_to(value[None], (peers, *value.shape)), axis, 0, 0, tiled=True
    )


def over_copies(value, axis):
    everything = copy_for_each(value, axis)
    return jnp.sum(everything, axis=0)


def together(arrays, axis):
    ends = [0]
    for a in arrays:
        ends.append(ends[-1] + a.size)
    running = over_copies(jnp.concatenate([a.ravel() for a in arrays]), axis)
    return tuple((running[b:e].reshape(a.shape) for a, b, e in zip(arrays, ends, ends[1:])))


def rope_tables(positions, width, shards, shard):
    q_width = MODEL_WIDTH // shards
    k_width = KV // shards
    offset = jnp.arange(width, dtype=jnp.int32)
    is_query = offset < q_width
    is_key = jnp.logical_and(offset >= q_width, offset < q_width + k_width)
    dimension = jnp.where(
        is_query, (shard * q_width + offset) % HEAD, (shard * k_width + offset - q_width) % HEAD
    )
    pair = (dimension // 2).astype(jnp.float32)
    freq = jnp.float32(500000.0) ** (-2.0 * pair / HEAD)
    angle = positions.astype(jnp.float32)[:, None] * freq[None, :]
    rotate = jnp.logical_or(is_query, is_key)[None, :]
    cosine = jnp.where(rotate, jnp.cos(angle), jnp.float32(1.0))
    sine = jnp.where(rotate, jnp.sin(angle), jnp.float32(0.0))
    return (cosine[:, 0::2], sine[:, 0::2])


def on_device(
    normed_input, positions, fixed_weight_matrix, adapter_down_map, adapter_up_map, output_gradient
):
    rows, width = output_gradient.shape
    shards = lax.axis_size("tensor")
    shard = lax.axis_index("tensor")
    cosine, sine = rope_tables(positions, width, shards, shard)
    pairs = output_gradient.astype(jnp.float32).reshape(rows, width // 2, 2)
    first = pairs[:, :, 0] * cosine + pairs[:, :, 1] * sine
    second = pairs[:, :, 1] * cosine - pairs[:, :, 0] * sine
    unrotated_gradient = (
        jnp.stack([first, second], axis=2).reshape(rows, width).astype(jnp.bfloat16)
    )
    rank_input = jnp.dot(normed_input, adapter_down_map, preferred_element_type=jnp.float32)
    rank_gradient = jnp.dot(
        unrotated_gradient, adapter_up_map.T, preferred_element_type=jnp.float32
    )
    rank_input, rank_gradient = together((rank_input, rank_gradient), "tensor")
    low_xb = rank_input.astype(jnp.bfloat16)
    rank_gradient_up = rank_gradient.astype(jnp.bfloat16)
    factor = 2.0 / math.sqrt(rows * lax.axis_size("dp"))
    part_a = factor * jnp.dot(normed_input.T, rank_gradient_up, preferred_element_type=jnp.float32)
    part_b = factor * jnp.dot(low_xb.T, unrotated_gradient, preferred_element_type=jnp.float32)
    terms = jnp.dot(
        unrotated_gradient,
        lax.all_gather(fixed_weight_matrix, "dp", axis=0, tiled=True).T,
        preferred_element_type=jnp.float32,
    )
    base = lax.psum_scatter(terms, "tensor", scatter_dimension=1, tiled=True)
    adapter_branch = jnp.dot(
        rank_gradient_up, adapter_down_map.T, preferred_element_type=jnp.float32
    )
    grad_x = (base + 2.0 * adapter_branch).astype(jnp.bfloat16)
    grad_a, grad_b = together((part_a, part_b), "dp")
    return (grad_x, grad_a, grad_b)


def solution(mesh):
    placed = (
        P("dp", "tensor"),
        P("dp"),
        P("dp", "tensor"),
        P("tensor", None),
        P(None, "tensor"),
        P("dp", "tensor"),
    )
    return jax.shard_map(
        on_device,
        mesh=mesh,
        in_specs=placed,
        out_specs=(P("dp", "tensor"), P("tensor", None), P(None, "tensor")),
        check_vma=False,
    )
```

profile of v0, /device:TPU:1, one launch (start us, length us, event | category | flops | bytes accessed | tf_op | source)
XLA Modules:
  0.0 383.9 jit_solution(10950872956848355848)
XLA Ops:
  7.2 0.0 copy-start
  7.2 0.0 copy-start.4
  7.2 0.0 all-gather.2.cloned.1.call-start
  7.2 0.7 all-gather.2.cloned.1.call-update
  7.9 0.0 reduce-scatter.2.cloned.1.call-start
  8.0 0.0 copy-done.4
  8.0 11.1 %fusion = (f32[1024,640]{0,1:T(8,128)}, f32[1024,640]{0,1:T(8,128)}) fusion(f32[640]{0:T(1024)S(1)} %fusion.16, f32[1024]{0:T(1024)S(1)} %convert_element_type.26, pred[640]{0:T(1024)(128)(4,1)S(1)} %fusion.10), kind=kLoop, calls=%fused_computation.2 | loop fusion | flops 1966080 | bytes 5250176 | tf_op jit(solution)/shard_map/jit(_where)/select_n | solution.py:45
  19.1 5.1 %slice.57 = f32[1024,320]{0,1:T(8,128)S(1)} slice(f32[1024,640]{0,1:T(8,128)} %get-tuple-element.19), slice={[0:1024:1], [0:640:2]} | slice | bytes 2621440 | tf_op jit(solution)/shard_map/slice | solution.py:47
  24.3 3.0 copy.22
  27.2 4.4 %reshape.138 = f32[1024,320,2]{0,2,1:T(2,128)} reshape(f32[1024,640]{0,1:T(8,128)} %copy.22) | data formatting | bytes 5242880 | tf_op jit(solution)/shard_map/reshape | solution.py:57
  31.6 6.5 %slice.55 = f32[1024,320]{0,1:T(8,128)} slice(f32[1024,640]{0,1:T(8,128)} %get-tuple-element.18), slice={[0:1024:1], [0:640:2]} | slice | bytes 2621440 | tf_op jit(solution)/shard_map/slice | solution.py:47
  38.2 0.0 copy-start.1
  38.2 4.9 %fusion.22 = (f32[1024,320,1]{0,2,1:T(1,128)S(1)}, f32[1024,320,1]{0,2,1:T(1,128)S(1)}) fusion(f32[1024,320,2]{0,2,1:T(2,128)} %reshape.138), kind=kLoop, calls=%fused_computation.48 | loop fusion | bytes 5242880 | tf_op jit(solution)/shard_map/slice | solution.py:58
  43.1 0.0 copy-done.1
  43.1 1.0 fusion.8
  44.1 0.1 pad_maximum_fusion
  44.3 2.4 copy.23
  46.7 3.2 convert_element_type.28
  49.9 90.7 %all-gather.2.cloned.1.call-done = bf16[8192,640]{1,0:T(8,128)(2,1)} async-done(((bf16[1024,640]{1,0:T(8,128)(2,1)}), bf16[8192,640]{1,0:T(8,128)(2,1)}) %all-gather.2.cloned.1.call-update) | async-done | bytes 10485776 | tf_op jit(solution)/shard_map/all_gather | solution.py:75
  140.6 21.2 %fusion.24 = f32[1024,8192]{1,0:T(8,128)} fusion(bf16[1024,640]{0,1:T(8,128)(2,1)S(1)} %convert_element_type.28, bf16[8192,640]{1,0:T(8,128)(2,1)} %all-gather.2.cloned.1.call-done), kind=kOutput, calls=%fused_computation.50 | convolution fusion | flops 10737418240 | bytes 45350912 | tf_op jit(solution)/shard_map/dot_general | solution.py:73
  161.8 0.0 copy-start.3
  161.8 0.0 reduce-scatter.2.cloned.1.call-update
  161.8 0.7 copy-done.3
  162.5 0.0 copy-start.2
  162.5 0.6 fusion.26
  163.1 0.2 reshape.133
  163.3 0.0 copy-done
  163.3 0.0 copy-done.2
  163.3 0.4 fusion.25
  163.7 0.2 reshape.132
  163.9 1.6 broadcast_in_dim.38
  165.5 44.0 %all_to_all.12 = f32[16,1,32768]{2,1,0:T(1,128)} all-to-all(f32[16,1,32768]{2,1,0:T(1,128)S(1)} %broadcast_in_dim.38), channel_id=1, replica_groups=mesh['dp'=8,'tensor'=16] {'tensor'}, dimensions={0} | all-to-all | bytes 4194304 | tf_op jit(solution)/shard_map/all_to_all | solution.py:14
  209.5 3.0 reduce_sum.18
  212.5 0.2 convert_element_type.29
  212.7 0.2 convert_element_type.31
  212.9 0.4 convolution_multiply_fusion
  213.4 0.3 fusion.6
  213.6 0.1 copy.27
  213.8 0.1 reshape.134
  213.9 0.3 broadcast_in_dim.39
  214.3 157.9 %all_to_all.13 = f32[8,1,18432]{2,1,0:T(1,128)S(1)} all-to-all(f32[8,1,18432]{2,1,0:T(1,128)S(1)} %broadcast_in_dim.39), channel_id=1, replica_groups=mesh['dp'=8,'tensor'=16] {'dp'}, dimensions={0} | all-to-all | bytes 1179648 | tf_op jit(solution)/shard_map/all_to_all | solution.py:14
  372.2 0.4 reduce_sum.19
  372.7 0.1 slice.61
  372.8 0.7 copy.29
  373.5 0.6 reshape.136
  374.1 0.0 reduce-scatter.2.cloned.1.call-done
  374.1 3.0 add_convert_fusion
  (9 shorter events, 0.1 us)
Async XLA Ops:
  7.2 156.1 %copy-start = (bf16[1024,512]{1,0:T(8,128)(2,1)S(1)}, bf16[1024,512]{1,0:T(8,128)(2,1)}, u32[]{:S(2)}) copy-start(bf16[1024,512]{1,0:T(8,128)(2,1)} %param.6) | copy-start | bytes 3145732
  7.2 0.8 copy-start.4
  7.2 133.4 %all-gather.2.cloned.1.call-start = ((), (), s32[]{:S(2)}) async-start(), calls=%async_computation.3 | async-start | bytes 11796480 | tf_op jit(solution)/shard_map/all_gather | solution.py:75
  7.9 366.2 %reduce-scatter.2.cloned.1.call-start = ((), (), s32[]{:S(2)}) async-start(), calls=%async_computation.4 | async-start | bytes 35651584 | tf_op jit(solution)/shard_map/reduce_scatter | solution.py:78
  38.2 4.9 %copy-start.1 = (f32[1024,320]{0,1:T(8,128)S(1)}, f32[1024,320]{0,1:T(8,128)}, u32[]{:S(2)}) copy-start(f32[1024,320]{0,1:T(8,128)} %slice.55) | copy-start | bytes 3932164
  161.8 0.7 copy-start.3
  162.5 0.8 copy-start.2
Sparse Core Ops, SparseCore 0:
  10.3 130.2 all-gather.1
  161.9 204.8 reduce-scatter.1
where the time goes:
time: 385 us; the launch traced here: 384 us
  blocking collectives  202 us (52%)
  waiting for transfers between devices  91.4 us (24%)
  local copies, waits for them, and re-layouts  34.8 us (9%)
  matrix products  25.8 us (7%)
  other arithmetic  15.7 us (4%)
  between operations  14.3 us (4%)
    all_to_all x2, blocking collectives, copy_for_each(): lax.all_to_all(jnp.broadcast_to(value[None], (peers, *value.shape)), axis...  202 us
    all_gather x1, waiting for transfers between devices, on_device(): lax.all_gather(fixed_weight_matrix, 'dp', axis=0, tiled=True)  90.7 us
    dot_general x1, matrix products, on_device(): jnp.dot(unrotated_gradient, lax.all_gather(fixed_weight_matrix, 'dp', axi...  21.2 us
    slice x2, local copies, waits for them, and re-layouts, rope_tables(): return (cosine[:, 0::2], sine[:, 0::2])  11.7 us
    select_n x1, other arithmetic, rope_tables(): cosine = jnp.where(rotate, jnp.cos(angle), jnp.float32(1.0))  11.1 us
  transfers between devices with their start and end apart: 2, of which 1 were waited for; matrix products, arithmetic and copies ran while one was open for 13% of the time, Pallas kernels for 0%

commit v1 on v0

--- a/solution.py
+++ b/solution.py
@@ -72,7 +72,10 @@
     part_b = factor * jnp.dot(low_xb.T, unrotated_gradient, preferred_element_type=jnp.float32)
     terms = jnp.dot(
         unrotated_gradient,
-        lax.all_gather(fixed_weight_matrix, "dp", axis=0, tiled=True).T,
+        jnp.concatenate(
+            lax.all_to_all(jnp.stack([fixed_weight_matrix] * lax.axis_size("dp")), "dp", 0, 0),
+            axis=0,
+        ).T,
         preferred_element_type=jnp.float32,
     )
     base = lax.psum_scatter(terms, "tensor", scatter_dimension=1, tiled=True)

time: 385 us -> 424 us (1.10)
  the two profiles are of different devices: /device:TPU:1 before, /device:TPU:25 now
where the time goes in v1:
time: 424 us; the launch traced here: 423 us
  blocking collectives  206 us (49%)
  waiting for transfers between devices  113 us (27%)
  local copies, waits for them, and re-layouts  40.8 us (10%)
  matrix products  25.8 us (6%)
  other arithmetic  15.7 us (4%)
  between operations  14.2 us (3%)
  starting transfers between devices  7.58 us (2%)
    all_to_all x2, blocking collectives, copy_for_each(): lax.all_to_all(jnp.broadcast_to(value[None], (peers, *value.shape)), axis...  206 us
    all_to_all x1, waiting for transfers between devices, on_device(): lax.all_to_all(jnp.stack([fixed_weight_matrix] * lax.axis_size('dp')), 'd...  113 us
    dot_general x1, matrix products, on_device(): jnp.dot(unrotated_gradient, jnp.concatenate(lax.all_to_all(jnp.stack([fix...  21.2 us
    slice x2, local copies, waits for them, and re-layouts, rope_tables(): return (cosine[:, 0::2], sine[:, 0::2])  11.6 us
    select_n x1, other arithmetic, rope_tables(): sine = jnp.where(rotate, jnp.sin(angle), jnp.float32(0.0))  11.1 us
  transfers between devices with their start and end apart: 2, of which 1 were waited for; matrix products, arithmetic and copies ran while one was open for 12% of the time, Pallas kernels for 0%

profile of v1, /device:TPU:25, one launch (start us, length us, event | category | flops | bytes accessed | tf_op | source)
XLA Modules:
  0.0 423.0 jit_solution(10203084942013119209)
XLA Ops:
  7.2 0.0 copy-start
  7.2 6.2 %stack.11 = bf16[8,1024,640]{2,1,0:T(8,128)(2,1)} broadcast(bf16[1024,640]{1,0:T(8,128)(2,1)} %param.8), dimensions={1,2} | broadcast | bytes 11796480 | tf_op jit(solution)/shard_map/stack | solution.py:76
  13.4 0.0 copy-start.4
  13.4 7.6 %all-to-all-start = ((bf16[8,1024,640]{2,1,0:T(8,128)(2,1)}), bf16[8,1024,640]{2,1,0:T(8,128)(2,1)}, u32[]{:S(2)}, u32[]{:S(2)}) async-start(bf16[8,1024,640]{2,1,0:T(8,128)(2,1)} %stack.11), calls=%async_computation | async-start | bytes 20971520 | tf_op jit(solution)/shard_map/all_to_all | solution.py:76
  20.9 0.0 reduce-scatter.2.cloned.1.call-start
  21.0 0.0 copy-done.4
  21.0 11.1 %fusion.1 = (f32[1024,640]{0,1:T(8,128)}, f32[1024,640]{0,1:T(8,128)}) fusion(f32[640]{0:T(1024)S(1)} %fusion.14, f32[1024]{0:T(1024)S(1)} %convert_element_type.35, pred[640]{0:T(1024)(128)(4,1)S(1)} %fusion.8), kind=kLoop, calls=%fused_computation.3 | loop fusion | flops 1966080 | bytes 5250176 | tf_op jit(solution)/shard_map/jit(_where)/select_n | solution.py:46
  32.1 5.1 %slice.57 = f32[1024,320]{0,1:T(8,128)S(1)} slice(f32[1024,640]{0,1:T(8,128)} %get-tuple-element.18), slice={[0:1024:1], [0:640:2]} | slice | bytes 2621440 | tf_op jit(solution)/shard_map/slice | solution.py:47
  37.1 6.5 %slice.55 = f32[1024,320]{0,1:T(8,128)} slice(f32[1024,640]{0,1:T(8,128)} %get-tuple-element.19), slice={[0:1024:1], [0:640:2]} | slice | bytes 2621440 | tf_op jit(solution)/shard_map/slice | solution.py:47
  43.7 2.9 copy.22
  46.6 4.4 %reshape.151 = f32[1024,320,2]{0,2,1:T(2,128)} reshape(f32[1024,640]{0,1:T(8,128)} %copy.22) | data formatting | bytes 5242880 | tf_op jit(solution)/shard_map/reshape | solution.py:57
  51.0 0.0 copy-start.1
  51.0 4.9 %fusion.20 = (f32[1024,320,1]{0,2,1:T(1,128)S(1)}, f32[1024,320,1]{0,2,1:T(1,128)S(1)}) fusion(f32[1024,320,2]{0,2,1:T(2,128)} %reshape.151), kind=kLoop, calls=%fused_computation.46 | loop fusion | bytes 5242880 | tf_op jit(solution)/shard_map/slice | solution.py:58
  55.9 0.0 copy-done.1
  55.9 1.0 fusion.3
  56.9 0.1 maximum_convert_fusion
  57.1 2.4 copy.23
  59.5 3.2 convert_element_type.38
  62.7 113.2 %all-to-all-done = bf16[8,1024,640]{2,1,0:T(8,128)(2,1)} async-done(((bf16[8,1024,640]{2,1,0:T(8,128)(2,1)}), bf16[8,1024,640]{2,1,0:T(8,128)(2,1)}, u32[]{:S(2)}, u32[]{:S(2)}) %all-to-all-start) | async-done | bytes 10485792 | tf_op jit(solution)/shard_map/all_to_all | solution.py:76
  175.8 21.2 %fusion.22 = f32[1024,8192]{1,0:T(8,128)} fusion(bf16[1024,640]{0,1:T(8,128)(2,1)S(1)} %convert_element_type.38, bf16[8192,640]{1,0:T(8,128)(2,1)} %bitcast.2), kind=kOutput, calls=%fused_computation.48 | convolution fusion | flops 10737418240 | bytes 45350912 | tf_op jit(solution)/shard_map/dot_general | solution.py:73
  197.0 0.0 copy-start.3
  197.0 0.0 reduce-scatter.2.cloned.1.call-update
  197.1 0.7 copy-done.3
  197.8 0.0 copy-start.2
  197.8 0.6 fusion.24
  198.3 0.2 reshape.146
  198.5 0.0 copy-done
  198.5 0.0 copy-done.2
  198.5 0.4 fusion.23
  198.9 0.2 reshape.145
  199.2 1.6 broadcast_in_dim.38
  200.8 43.9 %all_to_all.17 = f32[16,1,32768]{2,1,0:T(1,128)} all-to-all(f32[16,1,32768]{2,1,0:T(1,128)S(1)} %broadcast_in_dim.38), channel_id=1, replica_groups=mesh['dp'=8,'tensor'=16] {'tensor'}, dimensions={0} | all-to-all | bytes 4194304 | tf_op jit(solution)/shard_map/all_to_all | solution.py:14
  244.7 3.0 reduce_sum.18
  247.7 0.2 convert_element_type.39
  247.9 0.2 convert_element_type.41
  248.1 0.4 convolution_multiply_fusion
  248.6 0.3 fusion.6
  248.8 0.1 copy.27
  249.0 0.1 reshape.147
  249.1 0.3 broadcast_in_dim.39
  249.4 161.8 %all_to_all.18 = f32[8,1,18432]{2,1,0:T(1,128)S(1)} all-to-all(f32[8,1,18432]{2,1,0:T(1,128)S(1)} %broadcast_in_dim.39), channel_id=1, replica_groups=mesh['dp'=8,'tensor'=16] {'dp'}, dimensions={0} | all-to-all | bytes 1179648 | tf_op jit(solution)/shard_map/all_to_all | solution.py:14
  411.3 0.4 reduce_sum.19
  411.7 0.1 slice.61
  411.9 0.7 copy.29
  412.6 0.6 reshape.149
  413.2 0.0 reduce-scatter.2.cloned.1.call-done
  413.2 3.0 add_convert_fusion
  (9 shorter events, 0.1 us)
Async XLA Ops:
  7.2 191.4 %copy-start = (bf16[1024,512]{1,0:T(8,128)(2,1)S(1)}, bf16[1024,512]{1,0:T(8,128)(2,1)}, u32[]{:S(2)}) copy-start(bf16[1024,512]{1,0:T(8,128)(2,1)} %param.6) | copy-start | bytes 3145732
  13.4 7.6 %copy-start.4 = (s32[1024]{0:T(1024)S(1)}, s32[1024]{0:T(1024)}, u32[]{:S(2)}) copy-start(s32[1024]{0:T(1024)} %param.7) | copy-start | bytes 12292
  13.4 162.5 %all-to-all-start = ((bf16[8,1024,640]{2,1,0:T(8,128)(2,1)}), bf16[8,1024,640]{2,1,0:T(8,128)(2,1)}, u32[]{:S(2)}, u32[]{:S(2)}) async-start(bf16[8,1024,640]{2,1,0:T(8,128)(2,1)} %stack.11), calls=%async_computation | async-start | bytes 20971520 | tf_op jit(solution)/shard_map/all_to_all | solution.py:76
  20.9 392.3 %reduce-scatter.2.cloned.1.call-start = ((), (), s32[]{:S(2)}) async-start(), calls=%async_computation.4 | async-start | bytes 35651584 | tf_op jit(solution)/shard_map/reduce_scatter | solution.py:81
  51.0 4.9 %copy-start.1 = (f32[1024,320]{0,1:T(8,128)S(1)}, f32[1024,320]{0,1:T(8,128)}, u32[]{:S(2)}) copy-start(f32[1024,320]{0,1:T(8,128)} %slice.55) | copy-start | bytes 3932164
  197.0 0.7 copy-start.3
  197.8 0.8 copy-start.2
Sparse Core Ops, SparseCore 0:
  197.2 208.3 reduce-scatter.1
